TPU v7x, 256 devices: a whole 4x4x8 slice. The times are simulated.
256 devices in a mesh: grp: 4 (over z_hi), freq: 64 (over z_lo, y, x, core).
Axes of the slice: x: 4, y: 4, z: 8 (z_hi: 4, z_lo: 2; z = z_hi * 2 + z_lo), core: 2. Of those that a mesh axis runs over, the one named last changes fastest.
Arguments:
- sources: bfloat16 [1024, 262144], P('freq', 'grp'), may hold values from -6 to 6
- panel_pos: float32 [3, 262144], P(None, 'grp'), may hold values from -1 to 1
- panel_blade: int32 [262144], P('grp'), may hold values from 0 to 3
- observer_table: float32 [3, 2048], replicated, may hold values from -8 to 8, as said below
- observer_index: int32 [32], replicated, may hold values from 0 to 2047
Outputs:
- spectra: float32 [512, 4, 2, 32], P('freq', 'grp')
Inputs may be any that keep to these rules, and one draw needn't show every extreme that they name: `observer_table`: each observer lies 3 to 8 units from the anchor (0, 0, 0).
All inputs are finite; a program needn't handle non-finite values.
Results may differ from a plain program's by a relative error of at most 0.0047.
Values may be sent and summed in bfloat16 or wider, within the bound.
No kernel may reach another device: no remote copies, remote signals or barrier semaphores. Data moves between devices by JAX's collectives and lax.ppermute only.
A program may use at most 64 MiB of HBM per device.

v0:
```python
import math
import jax
import jax.numpy as jnp
from jax import lax
from jax.sharding import PartitionSpec as P

NT = 1024
NF = 512
NCOMP = 4
wave_step = 0.04


def over_pieces(x, axis):
    return lax.all_gather(x, axis).sum(0)


def transform_table():
    row_index = jnp.arange(2 * NF, dtype=jnp.int32)
    samples = jnp.arange(NT, dtype=jnp.int32)
    frequency = row_index // 2
    parity = row_index % 2
    turn_count = frequency[:, None] * samples[None, :] % NT
    angle_table = 2.0 * math.pi / NT * turn_count.astype(jnp.float32)
    values = jnp.where(parity[:, None] == 0, jnp.cos(angle_table), -jnp.sin(angle_table))
    return (values / math.sqrt(NT)).astype(jnp.bfloat16)


def distances(positions, observers):
    offset_x = observers[0][:, None] - positions[0][None, :]
    offset_y = observers[1][:, None] - positions[1][None, :]
    offset_z = observers[2][:, None] - positions[2][None, :]
    return jnp.sqrt(offset_x * offset_x + offset_y * offset_y + offset_z * offset_z)


def blade_masks(blades):
    return (blades[None, :] == jnp.arange(NCOMP, dtype=jnp.int32)[:, None]).astype(jnp.bfloat16)


def frequency_term(frequency, spectrum_pair, blade_mask, distance, amplitude):
    wavenumber = wave_step * frequency.astype(jnp.float32)
    phase_angle = wavenumber * distance
    green_matrix = jnp.concatenate(
        [jnp.cos(phase_angle) * amplitude, -jnp.sin(phase_angle) * amplitude], axis=0
    ).astype(jnp.bfloat16)
    weighted = jnp.concatenate(
        [spectrum_pair[0][None, :] * blade_mask, spectrum_pair[1][None, :] * blade_mask], axis=0
    )
    product = lax.dot_general(
        weighted, green_matrix, (((1,), (1,)), ((), ())), preferred_element_type=jnp.float32
    )
    blade_count = blade_mask.shape[0]
    observer_count = distance.shape[0]
    real_part = product[:blade_count, :observer_count] - product[blade_count:, observer_count:]
    imag_part = product[:blade_count, observer_count:] + product[blade_count:, :observer_count]
    return jnp.stack([real_part, imag_part], axis=1)


def body(sources, panel_pos, panel_blade, observer_table, observer_index):
    freq_share = NF // lax.axis_size("freq")
    position = lax.axis_index("freq")
    observers = observer_table[:, observer_index]
    dft_table = transform_table()
    exchanged = lax.all_to_all(sources, "freq", split_axis=1, concat_axis=0, tiled=True)
    spectrum = jnp.dot(dft_table, exchanged, preferred_element_type=jnp.float32).astype(
        jnp.bfloat16
    )
    received = lax.all_to_all(spectrum, "freq", split_axis=0, concat_axis=1, tiled=True)
    spectra_pairs = received.reshape(freq_share, 2, received.shape[1])
    distance = distances(panel_pos, observers)
    amplitude = 0.25 / (math.pi * distance)
    blade_mask = blade_masks(panel_blade)
    frequencies = position * freq_share + jnp.arange(freq_share, dtype=jnp.int32)

    def per_frequency(element):
        return frequency_term(element[0], element[1], blade_mask, distance, amplitude)

    partial_value = lax.map(per_frequency, (frequencies, spectra_pairs))
    summed = over_pieces(partial_value, "grp")
    blade_share = NCOMP // lax.axis_size("grp")
    return lax.dynamic_slice_in_dim(summed, lax.axis_index("grp") * blade_share, blade_share, 1)


def solution(mesh):
    in_specs = (P("freq", "grp"), P(None, "grp"), P("grp"), P(), P())
    out_specs = P("freq", "grp", None, None)
    return jax.shard_map(body, mesh=mesh, in_specs=in_specs, out_specs=out_specs, check_vma=False)
```

profile of v0, /device:TPU:2, one launch (start us, length us, event | category | flops | bytes accessed | tf_op | source)
XLA Modules:
  0.0 451.5 jit_solution(7879830638706427243)
XLA Ops:
  0.0 3.2 copy.19
  3.2 9.4 %all-to-all-start = ((bf16[16,64,1024]{2,0,1:T(8,128)(2,1)}), bf16[16,64,1024]{2,0,1:T(8,128)(2,1)S(1)}, u32[]{:S(2)}, u32[]{:S(2)}) async-start(bf16[16,64,1024]{2,0,1:T(8,128)(2,1)} %bitcast.24), calls=%async_computation | async-start | bytes 4194304 | tf_op jit(solution)/shard_map/all_to_all | solution.py:63
  12.6 27.8 %all-to-all-done = bf16[16,64,1024]{2,0,1:T(8,128)(2,1)S(1)} async-done(((bf16[16,64,1024]{2,0,1:T(8,128)(2,1)}), bf16[16,64,1024]{2,0,1:T(8,128)(2,1)S(1)}, u32[]{:S(2)}, u32[]{:S(2)}) %all-to-all-start) | async-done | bytes 2097184 | tf_op jit(solution)/shard_map/all_to_all | solution.py:63
  40.4 21.4 %fusion.32 = bf16[1024,1024]{1,0:T(8,128)(2,1)} fusion(bf16[1024,1024]{1,0:T(8,128)(2,1)S(1)} %bitcast.34, s32[1024]{0:T(1024)S(1)} %add_select_fusion.1, pred[1024]{0:T(1024)(128)(4,1)S(1)} %fusion.33), kind=kOutput, calls=%fused_computation.45 | convolution fusion | flops 2167406592 | bytes 4199424 | tf_op jit(solution)/shard_map/dot_general | solution.py:64
  61.8 7.3 %all-to-all-start.1 = ((bf16[64,16,1024]{2,1,0:T(8,128)(2,1)}), bf16[64,16,1024]{2,1,0:T(8,128)(2,1)S(1)}, u32[]{:S(2)}, u32[]{:S(2)}) async-start(bf16[64,16,1024]{2,1,0:T(8,128)(2,1)} %bitcast.33), calls=%async_computation.1 | async-start | bytes 4194304 | tf_op jit(solution)/shard_map/all_to_all | solution.py:67
  69.1 0.0 copy-done.1
  69.1 1.4 fusion.44
  70.6 0.4 copy.15
  71.0 0.6 gather_fusion
  71.6 0.2 slice_reduce_fusion
  71.8 25.2 %all-to-all-done.1 = bf16[64,16,1024]{2,1,0:T(8,128)(2,1)S(1)} async-done(((bf16[64,16,1024]{2,1,0:T(8,128)(2,1)}), bf16[64,16,1024]{2,1,0:T(8,128)(2,1)S(1)}, u32[]{:S(2)}, u32[]{:S(2)}) %all-to-all-start.1) | async-done | bytes 2097184 | tf_op jit(solution)/shard_map/all_to_all | solution.py:67
  97.0 2.5 copy.14
  99.5 4.9 %reshape.45 = bf16[8,2,65536]{2,1,0:T(2,128)(2,1)S(1)} reshape(bf16[16,64,1024]{2,1,0:T(8,128)(2,1)} %copy.14) | data formatting | bytes 4194304 | tf_op jit(solution)/shard_map/reshape | solution.py:68
  104.4 329.8 %while.12 = (s32[]{:T(128)}, f32[8,4,2,32]{3,1,2,0:T(4,128)S(1)}, bf16[8,2,65536]{2,1,0:T(2,128)(2,1)S(1)}, s32[8]{0:T(128)S(1)}, s32[65536]{0:T(1024)S(1)}, /*i...) while((s32[]{:T(128)}, f32[8,4,2,32]{3,1,2,0:T(4,128)S(1)}, ...), condition=%wide.region_1.2_spmd.clone.clone, body=%wide.region_0.1_spmd.clone.clone.sunk | while | flops 120324608 | bytes 20723280 | solution.py:77
  104.4 0.6 dynamic_slice.18
  105.6 1.4 dynamic-slice_reduce_fusion.3
  107.0 0.5 fusion.53
  107.5 35.8 %multiply_convert_fusion.7 = (bf16[32,65536]{1,0:T(8,128)(2,1)S(1)}, bf16[32,65536]{1,0:T(8,128)(2,1)S(1)}) fusion(f32[65536]{0:T(1024)S(1)} %get-tuple-element.290, f32[32]{0:T(128)S(1)} %get-tuple-element.291, f32[65536]{0:T(1024)S(1)} %get-tuple-element.288, f32[32]{0:T(128)S(1)} %get-tuple-element.289, f32[65536]{0:T(1024)S(1)} %get-tuple-element.286, ...), kind=kLoop, calls=%fused_computation.11.clone.1 | loop fusion | flops 33554432 | bytes 9175428 | tf_op jit(solution)/shard_map/convert
  143.3 2.3 fusion.54
  145.5 0.1 subtract_bitcast_fusion.2
  145.6 0.6 dynamic_slice.18
  146.8 1.4 dynamic-slice_reduce_fusion.3
  148.2 0.5 fusion.53
  148.7 35.8 %multiply_convert_fusion.7 = (bf16[32,65536]{1,0:T(8,128)(2,1)S(1)}, bf16[32,65536]{1,0:T(8,128)(2,1)S(1)}) fusion(f32[65536]{0:T(1024)S(1)} %get-tuple-element.290, f32[32]{0:T(128)S(1)} %get-tuple-element.291, f32[65536]{0:T(1024)S(1)} %get-tuple-element.288, f32[32]{0:T(128)S(1)} %get-tuple-element.289, f32[65536]{0:T(1024)S(1)} %get-tuple-element.286, ...), kind=kLoop, calls=%fused_computation.11.clone.1 | loop fusion | flops 33554432 | bytes 9175428 | tf_op jit(solution)/shard_map/convert
  184.5 2.3 fusion.54
  186.8 0.1 subtract_bitcast_fusion.2
  186.9 0.6 dynamic_slice.18
  188.0 1.4 dynamic-slice_reduce_fusion.3
  189.4 0.5 fusion.53
  189.9 35.8 %multiply_convert_fusion.7 = (bf16[32,65536]{1,0:T(8,128)(2,1)S(1)}, bf16[32,65536]{1,0:T(8,128)(2,1)S(1)}) fusion(f32[65536]{0:T(1024)S(1)} %get-tuple-element.290, f32[32]{0:T(128)S(1)} %get-tuple-element.291, f32[65536]{0:T(1024)S(1)} %get-tuple-element.288, f32[32]{0:T(128)S(1)} %get-tuple-element.289, f32[65536]{0:T(1024)S(1)} %get-tuple-element.286, ...), kind=kLoop, calls=%fused_computation.11.clone.1 | loop fusion | flops 33554432 | bytes 9175428 | tf_op jit(solution)/shard_map/convert
  225.7 2.3 fusion.54
  228.0 0.1 subtract_bitcast_fusion.2
  228.1 0.6 dynamic_slice.18
  229.2 1.4 dynamic-slice_reduce_fusion.3
  230.7 0.5 fusion.53
  231.1 35.8 %multiply_convert_fusion.7 = (bf16[32,65536]{1,0:T(8,128)(2,1)S(1)}, bf16[32,65536]{1,0:T(8,128)(2,1)S(1)}) fusion(f32[65536]{0:T(1024)S(1)} %get-tuple-element.290, f32[32]{0:T(128)S(1)} %get-tuple-element.291, f32[65536]{0:T(1024)S(1)} %get-tuple-element.288, f32[32]{0:T(128)S(1)} %get-tuple-element.289, f32[65536]{0:T(1024)S(1)} %get-tuple-element.286, ...), kind=kLoop, calls=%fused_computation.11.clone.1 | loop fusion | flops 33554432 | bytes 9175428 | tf_op jit(solution)/shard_map/convert
  266.9 2.3 fusion.54
  269.2 0.1 subtract_bitcast_fusion.2
  269.3 0.6 dynamic_slice.18
  270.5 1.4 dynamic-slice_reduce_fusion.3
  271.9 0.5 fusion.53
  272.4 35.8 %multiply_convert_fusion.7 = (bf16[32,65536]{1,0:T(8,128)(2,1)S(1)}, bf16[32,65536]{1,0:T(8,128)(2,1)S(1)}) fusion(f32[65536]{0:T(1024)S(1)} %get-tuple-element.290, f32[32]{0:T(128)S(1)} %get-tuple-element.291, f32[65536]{0:T(1024)S(1)} %get-tuple-element.288, f32[32]{0:T(128)S(1)} %get-tuple-element.289, f32[65536]{0:T(1024)S(1)} %get-tuple-element.286, ...), kind=kLoop, calls=%fused_computation.11.clone.1 | loop fusion | flops 33554432 | bytes 9175428 | tf_op jit(solution)/shard_map/convert
  308.2 2.3 fusion.54
  310.4 0.1 subtract_bitcast_fusion.2
  310.5 0.6 dynamic_slice.18
  311.7 1.4 dynamic-slice_reduce_fusion.3
  313.1 0.5 fusion.53
  313.6 35.8 %multiply_convert_fusion.7 = (bf16[32,65536]{1,0:T(8,128)(2,1)S(1)}, bf16[32,65536]{1,0:T(8,128)(2,1)S(1)}) fusion(f32[65536]{0:T(1024)S(1)} %get-tuple-element.290, f32[32]{0:T(128)S(1)} %get-tuple-element.291, f32[65536]{0:T(1024)S(1)} %get-tuple-element.288, f32[32]{0:T(128)S(1)} %get-tuple-element.289, f32[65536]{0:T(1024)S(1)} %get-tuple-element.286, ...), kind=kLoop, calls=%fused_computation.11.clone.1 | loop fusion | flops 33554432 | bytes 9175428 | tf_op jit(solution)/shard_map/convert
  349.4 2.3 fusion.54
  351.7 0.1 subtract_bitcast_fusion.2
  351.7 0.6 dynamic_slice.18
  352.9 1.4 dynamic-slice_reduce_fusion.3
  354.3 0.5 fusion.53
  354.8 35.8 %multiply_convert_fusion.7 = (bf16[32,65536]{1,0:T(8,128)(2,1)S(1)}, bf16[32,65536]{1,0:T(8,128)(2,1)S(1)}) fusion(f32[65536]{0:T(1024)S(1)} %get-tuple-element.290, f32[32]{0:T(128)S(1)} %get-tuple-element.291, f32[65536]{0:T(1024)S(1)} %get-tuple-element.288, f32[32]{0:T(128)S(1)} %get-tuple-element.289, f32[65536]{0:T(1024)S(1)} %get-tuple-element.286, ...), kind=kLoop, calls=%fused_computation.11.clone.1 | loop fusion | flops 33554432 | bytes 9175428 | tf_op jit(solution)/shard_map/convert
  390.6 2.3 fusion.54
  392.9 0.1 subtract_bitcast_fusion.2
  393.0 0.6 dynamic_slice.18
  394.1 1.4 dynamic-slice_reduce_fusion.3
  395.5 0.5 fusion.53
  396.0 35.8 %multiply_convert_fusion.7 = (bf16[32,65536]{1,0:T(8,128)(2,1)S(1)}, bf16[32,65536]{1,0:T(8,128)(2,1)S(1)}) fusion(f32[65536]{0:T(1024)S(1)} %get-tuple-element.290, f32[32]{0:T(128)S(1)} %get-tuple-element.291, f32[65536]{0:T(1024)S(1)} %get-tuple-element.288, f32[32]{0:T(128)S(1)} %get-tuple-element.289, f32[65536]{0:T(1024)S(1)} %get-tuple-element.286, ...), kind=kLoop, calls=%fused_computation.11.clone.1 | loop fusion | flops 33554432 | bytes 9175428 | tf_op jit(solution)/shard_map/convert
  431.8 2.3 fusion.54
  434.1 0.1 subtract_bitcast_fusion.2
  434.2 16.6 %all-gather = f32[32,4,2,32]{3,1,2,0:T(4,128)S(1)} all-gather(f32[8,4,2,32]{3,1,2,0:T(4,128)S(1)} %get-tuple-element.42), channel_id=2, replica_groups=mesh['grp'=4,'freq'=64] {'grp'}, dimensions={0}, use_global_device_ids=true | all-gather | bytes 40960 | tf_op jit(solution)/shard_map/all_gather | solution.py:14
  450.8 0.6 constant_dynamic-slice_fusion
  (28 shorter events, 0.2 us)
Async XLA Ops:
  3.2 37.2 %all-to-all-start = ((bf16[16,64,1024]{2,0,1:T(8,128)(2,1)}), bf16[16,64,1024]{2,0,1:T(8,128)(2,1)S(1)}, u32[]{:S(2)}, u32[]{:S(2)}) async-start(bf16[16,64,1024]{2,0,1:T(8,128)(2,1)} %bitcast.24), calls=%async_computation | async-start | bytes 4194304 | tf_op jit(solution)/shard_map/all_to_all | solution.py:63
  61.8 7.3 %copy-start.1 = (f32[3,65536]{1,0:T(4,128)S(1)}, f32[3,65536]{1,0:T(4,128)}, u32[]{:S(2)}) copy-start(f32[3,65536]{1,0:T(4,128)} %param.8) | copy-start | bytes 2359300
  61.8 8.8 %copy-start.5 = (f32[3,2048]{1,0:T(4,128)S(1)}, f32[3,2048]{1,0:T(4,128)}, u32[]{:S(2)}) copy-start(f32[3,2048]{1,0:T(4,128)} %param.10) | copy-start | bytes 73732
  61.8 9.2 %copy-start.6 = (s32[32]{0:T(128)S(1)}, s32[32]{0:T(128)}, u32[]{:S(2)}) copy-start(s32[32]{0:T(128)} %param.11) | copy-start | bytes 388
  61.8 35.2 %all-to-all-start.1 = ((bf16[64,16,1024]{2,1,0:T(8,128)(2,1)}), bf16[64,16,1024]{2,1,0:T(8,128)(2,1)S(1)}, u32[]{:S(2)}, u32[]{:S(2)}) async-start(bf16[64,16,1024]{2,1,0:T(8,128)(2,1)} %bitcast.33), calls=%async_computation.1 | async-start | bytes 4194304 | tf_op jit(solution)/shard_map/all_to_all | solution.py:67
  97.0 7.4 %copy-start = (s32[65536]{0:T(1024)S(1)}, s32[65536]{0:T(1024)}, u32[]{:S(2)}) copy-start(s32[65536]{0:T(1024)} %param.9) | copy-start | bytes 786436
  97.0 7.4 %copy-start.2 = (f32[1,65536]{1,0:T(1,128)S(1)}, f32[1,65536]{1,0:T(1,128)}, u32[]{:S(2)}) copy-start(f32[1,65536]{1,0:T(1,128)} %get-tuple-element.165) | copy-start | bytes 786436
  97.0 7.4 %copy-start.3 = (f32[1,65536]{1,0:T(1,128)S(1)}, f32[1,65536]{1,0:T(1,128)}, u32[]{:S(2)}) copy-start(f32[1,65536]{1,0:T(1,128)} %get-tuple-element.166) | copy-start | bytes 786436
  97.0 7.4 %copy-start.4 = (f32[1,65536]{1,0:T(1,128)S(1)}, f32[1,65536]{1,0:T(1,128)}, u32[]{:S(2)}) copy-start(f32[1,65536]{1,0:T(1,128)} %get-tuple-element.167) | copy-start | bytes 786436
where the time goes:
time: 452 us; the launch traced here: 451 us
  other arithmetic  291 us (64%)
  waiting for transfers between devices  53 us (12%)
  matrix products  39.5 us (9%)
  local copies, waits for them, and re-layouts  29.8 us (7%)
  starting transfers between devices  16.7 us (4%)
  blocking collectives  16.6 us (4%)
  loops' own time  4.72 us (1%)
    another operation x8, other arithmetic  286 us
    all_to_all x1, waiting for transfers between devices, body(): lax.all_to_all(sources, 'freq', split_axis=1, concat_axis=0, tiled=True)  27.8 us
    all_to_all x1, waiting for transfers between devices, body(): lax.all_to_all(spectrum, 'freq', split_axis=0, concat_axis=1, tiled=True)  25.2 us
    dot_general x1, matrix products, body(): jnp.dot(dft_table, exchanged, preferred_element_type=jnp.float32)  21.4 us
    dot_general x8, matrix products, frequency_term(): lax.dot_general(weighted, green_matrix, (((1,), (1,)), ((), ())), preferr...  18.1 us
    all_gather x1, blocking collectives, over_pieces(): return lax.all_gather(x, axis).sum(0)  16.6 us
    slice x8, local copies, waits for them, and re-layouts, frequency_term(): spectrum_pair[0][None, :] * blade_mask  11.3 us
    all_to_all x1, starting transfers between devices, body(): lax.all_to_all(sources, 'freq', split_axis=1, concat_axis=0, tiled=True)  9.37 us
  transfers between devices with their start and end apart: 2, of which 2 were waited for; matrix products, arithmetic and copies ran while one was open for 1% of the time, Pallas kernels for 0%

commit v1 on v0

--- a/solution.py
+++ b/solution.py
@@ -60,7 +60,10 @@
     position = lax.axis_index("freq")
     observers = observer_table[:, observer_index]
     dft_table = transform_table()
-    exchanged = lax.all_to_all(sources, "freq", split_axis=1, concat_axis=0, tiled=True)
+    exchanged = jnp.concatenate(
+        lax.all_to_all(jnp.stack(jnp.split(sources, lax.axis_size("freq"), axis=1)), "freq", 0, 0),
+        axis=0,
+    )
     spectrum = jnp.dot(dft_table, exchanged, preferred_element_type=jnp.float32).astype(
         jnp.bfloat16
     )

time: 452 us -> 542 us (1.20)
  local copies, waits for them, and re-layouts: 29.8 us -> 114 us
    unnamed x15 -> x76, local copies, waits for them, and re-layouts: 0.38 us -> 86.1 us
  transfers between devices with their start and end apart: 2 -> 2, of which waited for: 2 -> 2; matrix products, arithmetic and copies ran while one was open for 1% -> 0% of each run, Pallas kernels for 0% -> 0%
where the time goes in v1:
time: 542 us; the launch traced here: 537 us
  other arithmetic  291 us (54%)
  local copies, waits for them, and re-layouts  114 us (21%)
  waiting for transfers between devices  53.1 us (10%)
  matrix products  39.5 us (7%)
  starting transfers between devices  16.7 us (3%)
  blocking collectives  16.6 us (3%)
  loops' own time  5.76 us (1%)
    another operation x8, other arithmetic  286 us
    unnamed x76, local copies, waits for them, and re-layouts  86.1 us
    all_to_all x1, waiting for transfers between devices, body(): lax.all_to_all(jnp.stack(jnp.split(sources, lax.axis_size('freq'), axis=1...  27.8 us
    all_to_all x1, waiting for transfers between devices, body(): lax.all_to_all(spectrum, 'freq', split_axis=0, concat_axis=1, tiled=True)  25.3 us
    dot_general x1, matrix products, body(): jnp.dot(dft_table, exchanged, preferred_element_type=jnp.float32)  21.4 us
    dot_general x8, matrix products, frequency_term(): lax.dot_general(weighted, green_matrix, (((1,), (1,)), ((), ())), preferr...  18.1 us
    all_gather x1, blocking collectives, over_pieces(): return lax.all_gather(x, axis).sum(0)  16.6 us
    slice x8, local copies, waits for them, and re-layouts, frequency_term(): spectrum_pair[0][None, :] * blade_mask  11.3 us
  transfers between devices with their start and end apart: 2, of which 2 were waited for; matrix products, arithmetic and copies ran while one was open for 0% of the time, Pallas kernels for 0%

profile of v1, /device:TPU:2, one launch (start us, length us, event | category | flops | bytes accessed | tf_op | source)
XLA Modules:
  0.0 537.2 jit_solution(17654106578965600208)
XLA Ops:
  1.4 1.4 constant_dynamic-update-slice_fusion.62
  4.1 1.4 constant_dynamic-update-slice_fusion.60
  6.8 1.4 constant_dynamic-update-slice_fusion.58
  9.5 1.4 constant_dynamic-update-slice_fusion.56
  12.3 1.4 constant_dynamic-update-slice_fusion.54
  13.6 1.4 constant_dynamic-update-slice_fusion.53
  15.0 1.4 constant_dynamic-update-slice_fusion.52
  17.7 1.4 constant_dynamic-update-slice_fusion.50
  19.1 1.4 constant_dynamic-update-slice_fusion.49
  21.8 1.4 constant_dynamic-update-slice_fusion.47
  23.2 1.4 constant_dynamic-update-slice_fusion.46
  25.9 1.4 constant_dynamic-update-slice_fusion.44
  28.6 1.4 constant_dynamic-update-slice_fusion.42
  36.8 1.4 constant_dynamic-update-slice_fusion.36
  38.1 1.4 constant_dynamic-update-slice_fusion.35
  40.8 1.4 constant_dynamic-update-slice_fusion.33
  42.2 1.4 constant_dynamic-update-slice_fusion.32
  44.9 1.4 constant_dynamic-update-slice_fusion.30
  46.3 1.4 constant_dynamic-update-slice_fusion.29
  47.7 1.4 constant_dynamic-update-slice_fusion.28
  50.4 1.4 constant_dynamic-update-slice_fusion.26
  53.1 1.4 constant_dynamic-update-slice_fusion.24
  58.6 1.4 constant_dynamic-update-slice_fusion.20
  61.3 1.4 constant_dynamic-update-slice_fusion.18
  64.0 1.4 constant_dynamic-update-slice_fusion.16
  69.5 1.4 constant_dynamic-update-slice_fusion.12
  72.2 1.4 constant_dynamic-update-slice_fusion.10
  74.9 1.4 constant_dynamic-update-slice_fusion.8
  80.4 1.4 constant_dynamic-update-slice_fusion.4
  81.7 1.4 constant_dynamic-update-slice_fusion.3
  85.8 1.4 constant_dynamic-update-slice_fusion
  87.2 9.4 %all-to-all-start = ((bf16[64,16,1024]{2,1,0:T(8,128)(2,1)}), bf16[64,16,1024]{2,1,0:T(8,128)(2,1)S(1)}, u32[]{:S(2)}, u32[]{:S(2)}) async-start(bf16[64,16,1024]{2,1,0:T(8,128)(2,1)} %constant_dynamic-update-slice_fusion), calls=%async_computation | async-start | bytes 4194304 | tf_op jit(solution)/shard_map/all_to_all | solution.py:64
  96.6 27.8 %all-to-all-done = bf16[64,16,1024]{2,1,0:T(8,128)(2,1)S(1)} async-done(((bf16[64,16,1024]{2,1,0:T(8,128)(2,1)}), bf16[64,16,1024]{2,1,0:T(8,128)(2,1)S(1)}, u32[]{:S(2)}, u32[]{:S(2)}) %all-to-all-start) | async-done | bytes 2097184 | tf_op jit(solution)/shard_map/all_to_all | solution.py:64
  124.4 21.4 %fusion.32 = bf16[1024,1024]{1,0:T(8,128)(2,1)} fusion(bf16[1024,1024]{1,0:T(8,128)(2,1)S(1)} %bitcast.155, s32[1024]{0:T(1024)S(1)} %add_select_fusion.1, pred[1024]{0:T(1024)(128)(4,1)S(1)} %fusion.33), kind=kOutput, calls=%fused_computation.44 | convolution fusion | flops 2167406592 | bytes 4199424 | tf_op jit(solution)/shard_map/dot_general | solution.py:67
  145.8 7.3 %all-to-all-start.1 = ((bf16[64,16,1024]{2,1,0:T(8,128)(2,1)}), bf16[64,16,1024]{2,1,0:T(8,128)(2,1)S(1)}, u32[]{:S(2)}, u32[]{:S(2)}) async-start(bf16[64,16,1024]{2,1,0:T(8,128)(2,1)} %bitcast.154), calls=%async_computation.1 | async-start | bytes 4194304 | tf_op jit(solution)/shard_map/all_to_all | solution.py:70
  155.7 25.3 %all-to-all-done.1 = bf16[64,16,1024]{2,1,0:T(8,128)(2,1)S(1)} async-done(((bf16[64,16,1024]{2,1,0:T(8,128)(2,1)}), bf16[64,16,1024]{2,1,0:T(8,128)(2,1)S(1)}, u32[]{:S(2)}, u32[]{:S(2)}) %all-to-all-start.1) | async-done | bytes 2097184 | tf_op jit(solution)/shard_map/all_to_all | solution.py:70
  181.0 2.5 copy.10
  183.5 5.0 reshape.46
  188.5 331.5 %while.12 = (s32[]{:T(128)}, f32[8,4,2,32]{3,1,2,0:T(4,128)S(1)}, bf16[8,2,65536]{2,1,0:T(2,128)(2,1)S(1)}, s32[8]{0:T(128)S(1)}, s32[65536]{0:T(1024)S(1)}, /*i...) while((s32[]{:T(128)}, f32[8,4,2,32]{3,1,2,0:T(4,128)S(1)}, ...), condition=%wide.region_1.2_spmd.clone.clone, body=%wide.region_0.1_spmd.clone.clone.sunk | while | flops 120324608 | bytes 20723280 | solution.py:80
  189.8 1.4 dynamic-slice_reduce_fusion.3
  191.7 35.8 %multiply_convert_fusion.7 = (bf16[32,65536]{1,0:T(8,128)(2,1)S(1)}, bf16[32,65536]{1,0:T(8,128)(2,1)S(1)}) fusion(f32[65536]{0:T(1024)S(1)} %get-tuple-element.290, f32[32]{0:T(128)S(1)} %get-tuple-element.291, f32[65536]{0:T(1024)S(1)} %get-tuple-element.288, f32[32]{0:T(128)S(1)} %get-tuple-element.289, f32[65536]{0:T(1024)S(1)} %get-tuple-element.286, ...), kind=kLoop, calls=%fused_computation.11.clone.1 | loop fusion | flops 33554432 | bytes 9175428 | tf_op jit(solution)/shard_map/convert
  227.5 2.3 fusion.54
  231.3 1.4 dynamic-slice_reduce_fusion.3
  233.2 35.8 %multiply_convert_fusion.7 = (bf16[32,65536]{1,0:T(8,128)(2,1)S(1)}, bf16[32,65536]{1,0:T(8,128)(2,1)S(1)}) fusion(f32[65536]{0:T(1024)S(1)} %get-tuple-element.290, f32[32]{0:T(128)S(1)} %get-tuple-element.291, f32[65536]{0:T(1024)S(1)} %get-tuple-element.288, f32[32]{0:T(128)S(1)} %get-tuple-element.289, f32[65536]{0:T(1024)S(1)} %get-tuple-element.286, ...), kind=kLoop, calls=%fused_computation.11.clone.1 | loop fusion | flops 33554432 | bytes 9175428 | tf_op jit(solution)/shard_map/convert
  269.0 2.3 fusion.54
  272.7 1.4 dynamic-slice_reduce_fusion.3
  274.6 35.8 %multiply_convert_fusion.7 = (bf16[32,65536]{1,0:T(8,128)(2,1)S(1)}, bf16[32,65536]{1,0:T(8,128)(2,1)S(1)}) fusion(f32[65536]{0:T(1024)S(1)} %get-tuple-element.290, f32[32]{0:T(128)S(1)} %get-tuple-element.291, f32[65536]{0:T(1024)S(1)} %get-tuple-element.288, f32[32]{0:T(128)S(1)} %get-tuple-element.289, f32[65536]{0:T(1024)S(1)} %get-tuple-element.286, ...), kind=kLoop, calls=%fused_computation.11.clone.1 | loop fusion | flops 33554432 | bytes 9175428 | tf_op jit(solution)/shard_map/convert
  310.4 2.3 fusion.54
  314.2 1.4 dynamic-slice_reduce_fusion.3
  316.1 35.8 %multiply_convert_fusion.7 = (bf16[32,65536]{1,0:T(8,128)(2,1)S(1)}, bf16[32,65536]{1,0:T(8,128)(2,1)S(1)}) fusion(f32[65536]{0:T(1024)S(1)} %get-tuple-element.290, f32[32]{0:T(128)S(1)} %get-tuple-element.291, f32[65536]{0:T(1024)S(1)} %get-tuple-element.288, f32[32]{0:T(128)S(1)} %get-tuple-element.289, f32[65536]{0:T(1024)S(1)} %get-tuple-element.286, ...), kind=kLoop, calls=%fused_computation.11.clone.1 | loop fusion | flops 33554432 | bytes 9175428 | tf_op jit(solution)/shard_map/convert
  351.9 2.3 fusion.54
  355.6 1.4 dynamic-slice_reduce_fusion.3
  357.5 35.8 %multiply_convert_fusion.7 = (bf16[32,65536]{1,0:T(8,128)(2,1)S(1)}, bf16[32,65536]{1,0:T(8,128)(2,1)S(1)}) fusion(f32[65536]{0:T(1024)S(1)} %get-tuple-element.290, f32[32]{0:T(128)S(1)} %get-tuple-element.291, f32[65536]{0:T(1024)S(1)} %get-tuple-element.288, f32[32]{0:T(128)S(1)} %get-tuple-element.289, f32[65536]{0:T(1024)S(1)} %get-tuple-element.286, ...), kind=kLoop, calls=%fused_computation.11.clone.1 | loop fusion | flops 33554432 | bytes 9175428 | tf_op jit(solution)/shard_map/convert
  393.3 2.3 fusion.54
  397.0 1.4 dynamic-slice_reduce_fusion.3
  398.9 35.8 %multiply_convert_fusion.7 = (bf16[32,65536]{1,0:T(8,128)(2,1)S(1)}, bf16[32,65536]{1,0:T(8,128)(2,1)S(1)}) fusion(f32[65536]{0:T(1024)S(1)} %get-tuple-element.290, f32[32]{0:T(128)S(1)} %get-tuple-element.291, f32[65536]{0:T(1024)S(1)} %get-tuple-element.288, f32[32]{0:T(128)S(1)} %get-tuple-element.289, f32[65536]{0:T(1024)S(1)} %get-tuple-element.286, ...), kind=kLoop, calls=%fused_computation.11.clone.1 | loop fusion | flops 33554432 | bytes 9175428 | tf_op jit(solution)/shard_map/convert
  434.7 2.3 fusion.54
  438.5 1.4 dynamic-slice_reduce_fusion.3
  440.4 35.8 %multiply_convert_fusion.7 = (bf16[32,65536]{1,0:T(8,128)(2,1)S(1)}, bf16[32,65536]{1,0:T(8,128)(2,1)S(1)}) fusion(f32[65536]{0:T(1024)S(1)} %get-tuple-element.290, f32[32]{0:T(128)S(1)} %get-tuple-element.291, f32[65536]{0:T(1024)S(1)} %get-tuple-element.288, f32[32]{0:T(128)S(1)} %get-tuple-element.289, f32[65536]{0:T(1024)S(1)} %get-tuple-element.286, ...), kind=kLoop, calls=%fused_computation.11.clone.1 | loop fusion | flops 33554432 | bytes 9175428 | tf_op jit(solution)/shard_map/convert
  476.2 2.3 fusion.54
  479.9 1.4 dynamic-slice_reduce_fusion.3
  481.8 35.8 %multiply_convert_fusion.7 = (bf16[32,65536]{1,0:T(8,128)(2,1)S(1)}, bf16[32,65536]{1,0:T(8,128)(2,1)S(1)}) fusion(f32[65536]{0:T(1024)S(1)} %get-tuple-element.290, f32[32]{0:T(128)S(1)} %get-tuple-element.291, f32[65536]{0:T(1024)S(1)} %get-tuple-element.288, f32[32]{0:T(128)S(1)} %get-tuple-element.289, f32[65536]{0:T(1024)S(1)} %get-tuple-element.286, ...), kind=kLoop, calls=%fused_computation.11.clone.1 | loop fusion | flops 33554432 | bytes 9175428 | tf_op jit(solution)/shard_map/convert
  517.6 2.3 fusion.54
  520.0 16.6 %all-gather = f32[32,4,2,32]{3,1,2,0:T(4,128)S(1)} all-gather(f32[8,4,2,32]{3,1,2,0:T(4,128)S(1)} %get-tuple-element.42), channel_id=2, replica_groups=mesh['grp'=4,'freq'=64] {'grp'}, dimensions={0}, use_global_device_ids=true | all-gather | bytes 40960 | tf_op jit(solution)/shard_map/all_gather | solution.py:14
  (89 shorter events, 58.1 us)
Async XLA Ops:
  87.2 37.2 %all-to-all-start = ((bf16[64,16,1024]{2,1,0:T(8,128)(2,1)}), bf16[64,16,1024]{2,1,0:T(8,128)(2,1)S(1)}, u32[]{:S(2)}, u32[]{:S(2)}) async-start(bf16[64,16,1024]{2,1,0:T(8,128)(2,1)} %constant_dynamic-update-slice_fusion), calls=%async_computation | async-start | bytes 4194304 | tf_op jit(solution)/shard_map/all_to_all | solution.py:64
  145.8 7.3 %copy-start.1 = (f32[3,65536]{1,0:T(4,128)S(1)}, f32[3,65536]{1,0:T(4,128)}, u32[]{:S(2)}) copy-start(f32[3,65536]{1,0:T(4,128)} %param.8) | copy-start | bytes 2359300
  145.8 8.7 %copy-start.4 = (f32[3,2048]{1,0:T(4,128)S(1)}, f32[3,2048]{1,0:T(4,128)}, u32[]{:S(2)}) copy-start(f32[3,2048]{1,0:T(4,128)} %param.10) | copy-start | bytes 73732
  145.8 35.2 %all-to-all-start.1 = ((bf16[64,16,1024]{2,1,0:T(8,128)(2,1)}), bf16[64,16,1024]{2,1,0:T(8,128)(2,1)S(1)}, u32[]{:S(2)}, u32[]{:S(2)}) async-start(bf16[64,16,1024]{2,1,0:T(8,128)(2,1)} %bitcast.154), calls=%async_computation.1 | async-start | bytes 4194304 | tf_op jit(solution)/shard_map/all_to_all | solution.py:70
  153.1 1.7 copy-start.5
  183.5 5.0 copy-start
  183.5 5.0 copy-start.2
  183.5 5.0 copy-start.3
